TPU v7x, 32 devices: a whole 2x2x4 slice. The times are simulated.
32 devices in a mesh: ens: 2 (over y), gy: 4 (over z), gx: 4 (over x, core).
Axes of the slice: x: 2, y: 2, z: 4, core: 2. Of those that a mesh axis runs over, the one named last changes fastest.
Arguments:
- velocity: float32 [2, 2, 1024, 1024], P('ens', None, 'gy', 'gx'), may hold values from -3 to 3
- stress: float32 [2, 3, 1024, 1024], P('ens', None, 'gy', 'gx'), may hold values from -3 to 3
- thickness: float32 [2, 1024, 1024], P('ens', 'gy', 'gx'), may hold values from 2 to 3
- concentration: float32 [2, 1024, 1024], P('ens', 'gy', 'gx'), may hold values from 0.97 to 1
- node_mass: float32 [2, 1024, 1024], P('ens', 'gy', 'gx'), may hold values from 1 to 1.5
- wind_stress: float32 [2, 2, 1024, 1024], P('ens', None, 'gy', 'gx'), may hold values from -3 to 3
- ocean_current: float32 [2, 2, 1024, 1024], P('ens', None, 'gy', 'gx'), may hold values from -2 to 2
- ocean_mask: int32 [1024, 1024], P('gy', 'gx'), may hold values 0 or 1
- ice_blocks: int32 [2, 32, 32], P('ens', 'gy', 'gx'), may hold values 0 or 1
Outputs:
- velocity_out: float32 [2, 2, 1024, 1024], P('ens', None, 'gy', 'gx')
- stress_out: float32 [2, 3, 1024, 1024], P('ens', None, 'gy', 'gx')
- ensemble_mean: float32 [3, 1024, 1024], P(None, ('gy', 'ens'), 'gx')
- ensemble_variance: float32 [3, 1024, 1024], P(None, ('gy', 'ens'), 'gx')
All inputs are finite; a program needn't handle non-finite values. No bound on the sum of `ocean_mask` or of `ice_blocks` on one device may be relied on, other than what follows from the above.
Results may differ from a plain program's by a relative error of at most 0.00002.
Values sent between devices are 32-bit elements; how exact they have to be, the bound alone decides.
A program may use at most 64 MiB of HBM per device.

v0:
```python
import functools

import jax
import jax.numpy as jnp
from jax import lax
from jax.experimental import pallas as pl
from jax.experimental.pallas import tpu as pltpu
from jax.sharding import PartitionSpec as P

SUBCYCLES = 16
BLOCK = 32

TIME_STEP = 0.5
RELAX_RATE = 0.25
ECCENTRICITY_SQUARED = 4.0
CORIOLIS_TOP = 1.0
STRENGTH_DECAY = 20.0

MESH = pl.DeviceIdType.MESH
LANES = 128
TINY = 1.1754944e-38
GAIN = 1.0 + RELAX_RATE

MARGIN = SUBCYCLES
EXTRA = 8
TOP = 8
LOW = TOP
MID = TOP + MARGIN
STEP = 16

PACKED = (
    ("u", MARGIN + 1), ("v", MARGIN + 1), ("plus", MARGIN), ("minus", MARGIN), ("twice", MARGIN),
    ("pressure", MARGIN), ("inertia", MARGIN),
    ("ge", MARGIN), ("gn", MARGIN), ("ce", MARGIN), ("cn", MARGIN),
)
WHOLE = 7
OFFSETS = []
for _i, (_, _w) in enumerate(PACKED):
    if _i == 0 or _i == WHOLE:
        OFFSETS.append(0)
    else:
        OFFSETS.append(OFFSETS[-1] + PACKED[_i - 1][1])
HALF = LANES // 2

OWN = 36
AT_LEFT = MARGIN
AT_RIGHT = MARGIN + OWN
AT_HALO = MARGIN + 2 * OWN
AT_END = AT_HALO + MARGIN + 1

MAIN_FIELDS = (
    "u", "v", "plus", "minus", "twice", "pressure", "inertia", "turning",
    "ge", "gn", "ce", "cn", "cae", "can", "active",
)


def lane_index(rows):
    return lax.broadcasted_iota(jnp.int32, (rows, LANES), 1)


def rolled(value, shift):
    shift = shift % LANES
    return value if shift == 0 else pltpu.roll(value, shift, 1)


def step_kernel(sizes, *refs):
    gx_count, gy_count, ens_count = sizes
    inputs, refs = refs[:9], refs[9:]
    (vel_out, stress_out, conc_out, landing), refs = refs[:4], refs[4:]
    (svel, sstress, sthick, sconc, smass, swind, scur, smask, sice, expand), refs = refs[:10], refs[10:]
    arrays, refs = refs[: len(MAIN_FIELDS)], refs[len(MAIN_FIELDS) :]
    (out_a, out_b, in_a, in_b, load_sem, send_y, recv_y, send_x, recv_x, send_d, recv_d, send_e, recv_e) = refs
    field = dict(zip(MAIN_FIELDS, arrays))
    stages = (svel, sstress, sthick, sconc, smass, swind, scur, smask)
    rows, cols = conc_out.shape
    main = cols // LANES
    tiles = main + 1
    high = MID + rows
    blocks = rows // BLOCK
    gx, gy, me = lax.axis_index("gx"), lax.axis_index("gy"), lax.axis_index("ens")
    right, left = lax.rem(gx + 1, gx_count), lax.rem(gx + gx_count - 1, gx_count)
    has_lo, has_hi = gy > 0, gy < gy_count - 1
    lower, upper = jnp.maximum(gy - 1, 0), jnp.minimum(gy + 1, gy_count - 1)
    peers = [lax.rem(me + step, ens_count) for step in range(1, ens_count)]

    barrier = pltpu.get_barrier_semaphore()

    def greet(**where):
        pl.semaphore_signal(barrier, inc=1, device_id=where, device_id_type=MESH)

    greet(gx=left)
    greet(gx=right)
    for peer in peers:
        greet(ens=peer)
    for there, row in ((has_lo, lower), (has_hi, upper)):
        @pl.when(there)
        def _(row=row):
            greet(gy=row)
            greet(gy=row, gx=left)
            greet(gy=row, gx=right)

    own = slice(MARGIN, MARGIN + rows)

    def at_rows(ref, where):
        return ref.at[:, where] if len(ref.shape) == 3 else ref.at[where]

    loads = [
        pltpu.make_async_copy(source, at_rows(stage, own), load_sem.at[number])
        for number, (source, stage) in enumerate(zip(inputs, stages))
    ]
    loads.append(pltpu.make_async_copy(inputs[8], sice.at[blocks : 2 * blocks], load_sem.at[8]))
    for each in loads:
        each.start()

    def remote(source, target, sends, receives, number, where):
        return pltpu.make_async_remote_copy(
            src_ref=source, dst_ref=target, send_sem=sends.at[number], recv_sem=receives.at[number],
            device_id=where, device_id_type=MESH,
        )

    down, up = [], []
    for number, (source, stage) in enumerate(zip(inputs, stages)):
        extra = EXTRA if number in (0, 7) else 0
        down.append(remote(
            at_rows(source, slice(0, MARGIN + extra)),
            at_rows(stage, slice(MARGIN + rows, 2 * MARGIN + rows + extra)),
            send_y, recv_y, number, {"gy": lower},
        ))
        up.append(remote(
            at_rows(source, slice(rows - MARGIN, rows)),
            at_rows(stage, slice(0, MARGIN)),
            send_y, recv_y, 9 + number, {"gy": upper},
        ))
    down.append(remote(inputs[8], sice.at[2 * blocks : 3 * blocks], send_y, recv_y, 8, {"gy": lower}))
    up.append(remote(inputs[8], sice.at[0:blocks], send_y, recv_y, 17, {"gy": upper}))

    others = has_lo.astype(jnp.int32) + has_hi.astype(jnp.int32)
    pl.semaphore_wait(barrier, 2 + (ens_count - 1) + 3 * others)

    @pl.when(has_lo)
    def _():
        for each in down:
            each.start()

    @pl.when(has_hi)
    def _():
        for each in up:
            each.start()

    for each in loads:
        each.wait()

    block_cols = sice.shape[1]
    spread = (
        lax.broadcasted_iota(jnp.int32, (block_cols, cols), 1) // BLOCK
        == lax.broadcasted_iota(jnp.int32, (block_cols, cols), 0)
    ).astype(jnp.float32)

    repeat = (
        lax.broadcasted_iota(jnp.int32, (8 * blocks, blocks), 0) // 8
        == lax.broadcasted_iota(jnp.int32, (8 * blocks, blocks), 1)
    ).astype(jnp.float32)

    def expand_ice(part):
        flags = sice[part * blocks : (part + 1) * blocks].astype(jnp.float32)
        flags = jnp.dot(repeat, flags, preferred_element_type=jnp.float32)
        expand[8 * part * blocks : 8 * (part + 1) * blocks] = jnp.dot(
            flags, spread, preferred_element_type=jnp.float32)

    def convert(start, count, ice_row):
        at = pl.ds(start, count)
        to = pl.ds(start + TOP, count)
        row = lax.broadcasted_iota(jnp.int32, (count, LANES), 0) + (gy * rows + (start - MARGIN))
        coriolis = CORIOLIS_TOP * (row.astype(jnp.float32) + 0.5) / (rows * gy_count)
        for t in range(main):
            c = slice(t * LANES, (t + 1) * LANES)
            present = jnp.concatenate([expand[pl.ds(ice_row, 8), c]] * (count // 8))
            alive = smask[at, c].astype(jnp.float32) * present
            field["active"][t, to] = alive
            field["u"][t, to] = svel[0, at, c] * alive
            field["v"][t, to] = svel[1, at, c] * alive
            one, two = sstress[0, at, c], sstress[1, at, c]
            field["plus"][t, to] = one + two
            field["minus"][t, to] = one - two
            field["twice"][t, to] = 2.0 * sstress[2, at, c]
            factor = RELAX_RATE * 0.5 / GAIN
            field["pressure"][t, to] = factor * sthick[at, c] * jnp.exp(-STRENGTH_DECAY * (1.0 - sconc[at, c]))
            heavy = smass[at, c]
            heavy = jnp.where(heavy == 0.0, 1.0, heavy)
            turn = coriolis * heavy
            ce, cn = scur[0, at, c], scur[1, at, c]
            field["inertia"][t, to] = heavy / TIME_STEP
            field["turning"][t, to] = turn
            field["ge"][t, to] = swind[0, at, c] + turn * cn
            field["gn"][t, to] = swind[1, at, c] - turn * ce
            field["ce"][t, to] = ce
            field["cn"][t, to] = cn
            field["cae"][t, to] = alive * ce
            field["can"][t, to] = alive * cn

    expand_ice(1)

    def convert_own(block, _):
        convert(pl.multiple_of(MARGIN + block * BLOCK, 8), BLOCK, pl.multiple_of(8 * (blocks + block), 8))
        return 0

    lax.fori_loop(0, blocks, convert_own, 0)

    def message(name, tile, at):
        value = field[name][tile, at]
        return value * field["active"][tile, at] if name == "inertia" else value

    def packed(fields, at, count):
        lanes = lane_index(count)
        east = jnp.zeros((count, LANES), jnp.float32)
        west = jnp.zeros((count, LANES), jnp.float32)
        for number in fields:
            name, width = PACKED[number]
            start = OFFSETS[number]
            here = jnp.logical_and(lanes >= start, lanes < start + width)
            east = jnp.where(here, rolled(message(name, main - 1, at), start - (LANES - MARGIN)), east)
            west = jnp.where(here, rolled(message(name, 0, at), start), west)
        return east, west

    whole, part = range(WHOLE), range(WHOLE, len(PACKED))

    def pack_own(block, _):
        start = pl.multiple_of(block * BLOCK, 8)
        east, west = packed(whole, pl.ds(MID + start, BLOCK), BLOCK)
        out_a[0, pl.ds(start, BLOCK)] = east
        out_a[1, pl.ds(start, BLOCK)] = west
        return 0

    lax.fori_loop(0, blocks, pack_own, 0)

    def pack_half(block, _):
        start = pl.multiple_of(block * BLOCK, 8)
        east, west = packed(part, pl.ds(MID + start, BLOCK), BLOCK)
        more_east, more_west = packed(part, pl.ds(MID + rows // 2 + start, BLOCK), BLOCK)
        second = lane_index(BLOCK) >= HALF
        out_b[0, pl.ds(start, BLOCK)] = jnp.where(second, rolled(more_east, HALF), east)
        out_b[1, pl.ds(start, BLOCK)] = jnp.where(second, rolled(more_west, HALF), west)
        return 0

    lax.fori_loop(0, blocks // 2, pack_half, 0)

    sides = (right, left)
    across, corner_lo, corner_hi = [], [], []
    half_rows = rows // 2
    for side, to in enumerate(sides):
        across.append(remote(
            out_a.at[side], in_a.at[side, MARGIN : MARGIN + rows], send_x, recv_x, 2 * side, {"gx": to}))
        across.append(remote(
            out_b.at[side], in_b.at[side, MARGIN : MARGIN + half_rows], send_x, recv_x, 2 * side + 1, {"gx": to}))
        lo, hi = {"gx": to, "gy": lower}, {"gx": to, "gy": upper}
        corner_lo.append(remote(
            out_a.at[side, 0 : MARGIN + EXTRA],
            in_a.at[side, MARGIN + rows : 2 * MARGIN + rows + EXTRA],
            send_d, recv_d, 4 * side, lo))
        corner_lo.append(remote(
            out_b.at[side, 0:MARGIN],
            in_b.at[side, MARGIN + half_rows : 2 * MARGIN + half_rows],
            send_d, recv_d, 4 * side + 1, lo))
        corner_hi.append(remote(
            out_a.at[side, rows - MARGIN : rows], in_a.at[side, 0:MARGIN],
            send_d, recv_d, 4 * side + 2, hi))
        corner_hi.append(remote(
            out_b.at[side, half_rows - MARGIN : half_rows], in_b.at[side, 0:MARGIN],
            send_d, recv_d, 4 * side + 3, hi))
    for each in across:
        each.start()

    @pl.when(has_lo)
    def _():
        for each in corner_lo:
            each.start()

    @pl.when(has_hi)
    def _():
        for each in corner_hi:
            each.start()

    @pl.when(has_lo)
    def _():
        for each in up:
            each.wait_recv()

    @pl.when(jnp.logical_not(has_lo))
    def _():
        for stage in stages:
            for index in range(stage.shape[0]) if len(stage.shape) == 3 else (None,):
                view = stage if index is None else stage.at[index]
                view[0:MARGIN] = jnp.zeros((MARGIN, cols), stage.dtype)
        sice[0:blocks] = jnp.zeros((blocks, block_cols), jnp.int32)

    @pl.when(has_hi)
    def _():
        for each in down:
            each.wait_recv()

    @pl.when(jnp.logical_not(has_hi))
    def _():
        for stage in stages:
            count = stage.shape[-2] - MARGIN - rows
            for index in range(stage.shape[0]) if len(stage.shape) == 3 else (None,):
                view = stage if index is None else stage.at[index]
                view[MARGIN + rows : MARGIN + rows + count] = jnp.zeros((count, cols), stage.dtype)
        sice[2 * blocks : 3 * blocks] = jnp.zeros((blocks, block_cols), jnp.int32)

    expand_ice(0)
    expand_ice(2)
    convert(0, MARGIN, 8 * (blocks - 1))
    convert(MARGIN + rows, MARGIN, 16 * blocks)
    beyond = slice(2 * MARGIN + rows, 2 * MARGIN + rows + EXTRA)
    past = slice(high + MARGIN, high + MARGIN + EXTRA)
    for t in range(main):
        c = slice(t * LANES, (t + 1) * LANES)
        alive = smask[beyond, c].astype(jnp.float32) * expand[16 * blocks : 16 * blocks + 8, c]
        field["u"][t, past] = svel[0, beyond, c] * alive
        field["v"][t, past] = svel[1, beyond, c] * alive

    for each in across:
        each.wait_recv()

    @pl.when(has_lo)
    def _():
        for each in corner_hi:
            each.wait_recv()

    @pl.when(jnp.logical_not(has_lo))
    def _():
        for side in range(2):
            in_a[side, 0:MARGIN] = jnp.zeros((MARGIN, LANES), jnp.float32)
            in_b[side, 0:MARGIN] = jnp.zeros((MARGIN, LANES), jnp.float32)

    @pl.when(has_hi)
    def _():
        for each in corner_lo:
            each.wait_recv()

    @pl.when(jnp.logical_not(has_hi))
    def _():
        for side in range(2):
            in_a[side, MARGIN + rows :] = jnp.zeros((MARGIN + EXTRA, LANES), jnp.float32)
            in_b[side, MARGIN + half_rows :] = jnp.zeros((MARGIN, LANES), jnp.float32)

    def strip_value(number, start, count, half_start, half_lane):
        name, width = PACKED[number]
        lanes = lane_index(count)
        at = pl.ds(start, count)
        if number < WHOLE:
            arrived, there, lane = in_a, pl.ds(start - TOP, count), OFFSETS[number]
        else:
            arrived, there, lane = in_b, pl.ds(half_start, count), OFFSETS[number] + half_lane
        value = jnp.where(lanes < AT_HALO, rolled(message(name, main - 1, at), AT_HALO - LANES),
                          rolled(arrived[1, there], AT_HALO - lane))
        value = jnp.where(lanes < AT_RIGHT, rolled(message(name, 0, at), AT_LEFT), value)
        value = jnp.where(lanes < AT_LEFT, rolled(arrived[0, there], -lane), value)
        return jnp.where(lanes < AT_HALO + width, value, 0.0)

    def strip_rows(start, count, half_start, half_lane):
        at = pl.ds(start, count)
        value = {
            name: strip_value(number, start, count, half_start, half_lane)
            for number, (name, _) in enumerate(PACKED)
        }
        row = lax.broadcasted_iota(jnp.int32, (count, LANES), 0) + (gy * rows + (start - MID))
        coriolis = CORIOLIS_TOP * (row.astype(jnp.float32) + 0.5) / (rows * gy_count)
        empty = value["inertia"] == 0.0
        alive = jnp.where(empty, 0.0, 1.0)
        heavy = jnp.where(empty, 1.0 / TIME_STEP, value["inertia"])
        value["inertia"] = heavy
        value["turning"] = coriolis * (heavy * TIME_STEP)
        value["active"] = alive
        value["cae"] = alive * value["ce"]
        value["can"] = alive * value["cn"]
        for name in MAIN_FIELDS:
            field[name][main, at] = value[name]

    for half in range(2):
        def strip_own(block, _, half=half):
            start = pl.multiple_of(block * BLOCK, 8)
            strip_rows(MID + half * half_rows + start, BLOCK, MARGIN + start, half * HALF)
            return 0

        lax.fori_loop(0, blocks // 2, strip_own, 0)
    strip_rows(LOW, MARGIN, 0, HALF)
    strip_rows(high, MARGIN, MARGIN + half_rows, 0)
    for number in range(2):
        field[PACKED[number][0]][main, past] = strip_value(number, high + MARGIN, EXTRA, 0, 0)
    for name in ("plus", "minus", "twice"):
        for t in range(tiles):
            field[name][t, 0:LOW] = jnp.zeros((LOW, LANES), jnp.float32)

    u, v, plus, minus, twice = (field[name] for name in ("u", "v", "plus", "minus", "twice"))
    lanes = lane_index(STEP)
    at_end, at_start = lanes == LANES - 1, lanes == 0

    def ahead(values):
        turned = [rolled(value, -1) for value in values]
        return [jnp.where(at_end, turned[(t + 1) % main], turned[t]) for t in range(main)] + turned[main:]

    def behind(values):
        turned = [rolled(value, 1) for value in values]
        return [jnp.where(at_start, turned[t - 1 if t else main - 1], turned[t]) for t in range(main)] + turned[main:]

    def gradients(start):
        add, sub, add_s, sub_s = [], [], [], []
        for t in range(tiles):
            u0, u1 = u[t, pl.ds(start, STEP)], u[t, pl.ds(start + 1, STEP)]
            v0, v1 = v[t, pl.ds(start, STEP)], v[t, pl.ds(start + 1, STEP)]
            a, b, c, d = u0 + u1, u1 - u0, v0 + v1, v1 - v0
            add.append(a + d)
            sub.append(a - d)
            add_s.append(b + c)
            sub_s.append(b - c)
        return add, sub, add_s, sub_s

    def stress_rows(start, growth):
        at = pl.ds(start, STEP)
        add, sub, add_s, sub_s = gradients(start)
        add_next, sub_next, shear_next = ahead(add), ahead(sub), ahead(add_s)
        for t in range(tiles):
            div = add_next[t] - sub[t]
            tension = sub_next[t] - add[t]
            shear = shear_next[t] + sub_s[t]
            square = div * div + (1.0 / ECCENTRICITY_SQUARED) * (tension * tension + shear * shear)
            inverse = lax.rsqrt(jnp.maximum(square, TINY))
            ratio = jnp.minimum(square * inverse, 1.0)
            force = field["pressure"][t, at] * growth
            weight = force * jnp.minimum(inverse, 1.0)
            quarter = weight * (1.0 / ECCENTRICITY_SQUARED)
            change = weight * div - force * ratio
            other = quarter * tension
            plus[t, at] = plus[t, at] + (change + other)
            minus[t, at] = minus[t, at] + (change - other)
            twice[t, at] = twice[t, at] + quarter * shear

    def velocity_rows(start, scale):
        at, before = pl.ds(start, STEP), pl.ds(start - 1, STEP)
        e_near, e_far, n_near, n_far = [], [], [], []
        for t in range(tiles):
            p1, p0 = plus[t, at], plus[t, before]
            m1, m0 = minus[t, at], minus[t, before]
            s1, s0 = twice[t, at], twice[t, before]
            a, d, b, e = p0 + p1, s1 - s0, s0 + s1, m1 - m0
            e_near.append(a + d)
            e_far.append(a - d)
            n_near.append(b + e)
            n_far.append(b - e)
        e_far, n_far = behind(e_far), behind(n_far)
        for t in range(tiles):
            de, dn = u[t, at] - field["ce"][t, at], v[t, at] - field["cn"][t, at]
            square = de * de + dn * dn
            drag = square * lax.rsqrt(jnp.maximum(square, TINY))
            heavy, turn = field["inertia"][t, at], field["turning"][t, at]
            diag = heavy + drag
            push_e = heavy * de + ((e_near[t] - e_far[t]) * scale + field["ge"][t, at])
            push_n = heavy * dn + ((n_near[t] - n_far[t]) * scale + field["gn"][t, at])
            inverse = lax.rsqrt(diag * diag + turn * turn)
            inverse = field["active"][t, at] * (inverse * inverse)
            u[t, at] = (diag * push_e + turn * push_n) * inverse + field["cae"][t, at]
            v[t, at] = (diag * push_n - turn * push_e) * inverse + field["can"][t, at]

    count = (high + MARGIN - LOW) // STEP

    def subcycle(_, carried):
        growth, scale = carried
        stress_rows(LOW, growth)

        def both(block, _):
            start = pl.multiple_of(LOW + block * STEP, 8)
            stress_rows(start, growth)
            velocity_rows(start - STEP, scale)
            return 0

        lax.fori_loop(1, count, both, 0)
        velocity_rows(LOW + (count - 1) * STEP, scale)
        return growth * GAIN, scale * (1.0 / GAIN)

    lax.fori_loop(0, SUBCYCLES, subcycle, (jnp.float32(GAIN), jnp.float32(0.25 / GAIN)))

    shrink = 0.5 * GAIN**-SUBCYCLES
    on_left, on_right = lanes < MARGIN, lanes >= LANES - MARGIN - 2

    def merged(values):
        values = list(values)
        values[0] = jnp.where(on_left, rolled(values[main], -AT_LEFT), values[0])
        values[main - 1] = jnp.where(on_right, rolled(values[main], LANES - AT_HALO), values[main - 1])
        return values[:main]

    def finish(block, _):
        start = pl.multiple_of(block * STEP, 8)
        here, at = pl.ds(MID + start, STEP), pl.ds(start, STEP)
        add, sub, _, _ = gradients(MID + start)
        add_next = ahead(add)
        div = merged([add_next[t] - sub[t] for t in range(tiles)])
        east, north, one, two, three = (
            merged([ref[t, here] for t in range(tiles)]) for ref in (u, v, plus, minus, twice)
        )
        for t in range(main):
            c = slice(t * LANES, (t + 1) * LANES)
            vel_out[0, at, c] = east[t]
            vel_out[1, at, c] = north[t]
            stress_out[0, at, c] = (one[t] + two[t]) * shrink
            stress_out[1, at, c] = (one[t] - two[t]) * shrink
            stress_out[2, at, c] = three[t] * shrink
            value = sconc[pl.ds(MARGIN + start, STEP), c]
            conc_out[at, c] = jnp.clip(value - value * (0.5 * div[t]), 0.0, 1.0)
        return 0

    lax.fori_loop(0, rows // STEP, finish, 0)

    share = rows // ens_count
    swaps = []
    for step, peer in enumerate(peers):
        part_of = pl.ds(pl.multiple_of(peer * share, 8), share)
        swaps.append(remote(
            conc_out.at[part_of], landing.at[step, 0], send_e, recv_e, 2 * step, {"ens": peer}))
        swaps.append(remote(
            vel_out.at[:, part_of], landing.at[step, 1:3], send_e, recv_e, 2 * step + 1, {"ens": peer}))
    for each in swaps:
        each.start()
    for each in across:
        each.wait_send()

    @pl.when(has_lo)
    def _():
        for each in down + corner_lo:
            each.wait_send()

    @pl.when(has_hi)
    def _():
        for each in up + corner_hi:
            each.wait_send()

    for each in swaps:
        each.wait_recv()
    for each in swaps:
        each.wait_send()


def write_kernel(count, vel, stress, conc, landing, vel_out, stress_out, mean_out, spread_out, mean, spread, sems):
    copies = [
        pltpu.make_async_copy(vel, vel_out, sems.at[0]),
        pltpu.make_async_copy(stress, stress_out, sems.at[1]),
    ]
    for each in copies:
        each.start()
    share = mean.shape[1]
    own = pl.ds(pl.multiple_of(lax.axis_index("ens") * share, 8), share)
    for f in range(3):
        values = [conc[own] if f == 0 else vel[f - 1, own]]
        values += [landing[step, f] for step in range(count - 1)]
        average = functools.reduce(jnp.add, values) / count
        mean[f] = average
        spread[f] = functools.reduce(jnp.add, [(v - average) * (v - average) for v in values]) / count
    more = [
        pltpu.make_async_copy(mean, mean_out, sems.at[2]),
        pltpu.make_async_copy(spread, spread_out, sems.at[3]),
    ]
    for each in more:
        each.start()
    for each in copies + more:
        each.wait()


def solution(mesh):
    gx_count, gy_count, ens_count = mesh.shape["gx"], mesh.shape["gy"], mesh.shape["ens"]
    f32 = jnp.float32

    def vmem(*shape, dtype=f32):
        return pltpu.VMEM(shape, dtype)

    def specs(count, space):
        return [pl.BlockSpec(memory_space=space)] * count

    def body(velocity, stress, thickness, concentration, node_mass, wind, current, mask, ice):
        rows, cols = mask.shape
        share = rows // ens_count
        tiles = cols // LANES + 1
        block_rows, block_cols = ice.shape[1:]
        tall = rows + 2 * MARGIN
        total = TOP + tall + EXTRA
        shape = lambda *dims: jax.ShapeDtypeStruct(dims, f32)
        dma = lambda count: pltpu.SemaphoreType.DMA((count,))
        state = pl.pallas_call(
            functools.partial(step_kernel, (gx_count, gy_count, ens_count)),
            name="subcycles",
            out_shape=(
                shape(2, rows, cols),
                shape(3, rows, cols),
                shape(rows, cols),
                shape(ens_count - 1, 3, share, cols),
            ),
            in_specs=specs(9, pltpu.HBM),
            out_specs=tuple(specs(4, pltpu.VMEM)),
            scratch_shapes=[
                vmem(2, tall + EXTRA, cols),
                vmem(3, tall, cols),
                vmem(tall, cols),
                vmem(tall, cols),
                vmem(tall, cols),
                vmem(2, tall, cols),
                vmem(2, tall, cols),
                vmem(tall + EXTRA, cols, dtype=jnp.int32),
                vmem(3 * block_rows, block_cols, dtype=jnp.int32),
                vmem(24 * block_rows, cols),
            ]
            + [vmem(tiles, total, LANES)] * len(MAIN_FIELDS)
            + [
                vmem(2, rows, LANES),
                vmem(2, rows // 2, LANES),
                vmem(2, tall + EXTRA, LANES),
                vmem(2, rows // 2 + 2 * MARGIN, LANES),
                dma(9), dma(18), dma(18), dma(4), dma(4), dma(8), dma(8),
                dma(2 * (ens_count - 1)), dma(2 * (ens_count - 1)),
            ],
            compiler_params=pltpu.CompilerParams(
                collective_id=0, has_side_effects=True, vmem_limit_bytes=24 << 20),
        )(*(pltpu.with_memory_space_constraint(each, pltpu.HBM) for each in (
            velocity[0], stress[0], thickness[0], concentration[0], node_mass[0], wind[0], current[0], mask, ice[0])))
        vel_out, stress_out, mean, spread = pl.pallas_call(
            functools.partial(write_kernel, ens_count),
            name="write",
            out_shape=(shape(2, rows, cols), shape(3, rows, cols), shape(3, share, cols), shape(3, share, cols)),
            in_specs=specs(4, pltpu.VMEM),
            out_specs=tuple(specs(4, pltpu.HBM)),
            scratch_shapes=[vmem(3, share, cols), vmem(3, share, cols), dma(4)],
            compiler_params=pltpu.CompilerParams(vmem_limit_bytes=4 << 20),
        )(*state)
        return vel_out[None], stress_out[None], mean, spread

    grid = P("ens", "gy", "gx")
    pair = P("ens", None, "gy", "gx")
    split = P(None, ("gy", "ens"), "gx")
    return jax.shard_map(
        body,
        mesh=mesh,
        in_specs=(pair, pair, grid, grid, grid, pair, pair, P("gy", "gx"), grid),
        out_specs=(pair, pair, split, split),
        check_vma=False,
    )
```

profile of v0, /device:TPU:0, one launch (start us, length us, event | category | flops | bytes accessed | tf_op | source)
XLA Modules:
  0.0 70.0 jit_solution(14840721879023346999)
XLA Ops:
  0.6 68.0 %subcycles.1 = (f32[2,256,256]{2,1,0:T(8,128)S(1)}, f32[3,256,256]{2,1,0:T(8,128)S(1)}, f32[256,256]{1,0:T(8,128)S(1)}, f32[1,3,128,256]{3,2,1,0:T(8,128)S(1)}) custom-call(f32[2,256,256]{2,1,0:T(8,128)} %bitcast.11, f32[3,256,256]{2,1,0:T(8,128)} %bitcast.10, f32[256,256]{1,0:T(8,128)} %bitcast.14, f32[256,256]{1,0:T(8,128)} %bitcast.15, ...), custom_call_target="tpu_custom_call" | custom-call | tf_op jit(solution)/shard_map/subcycles/pallas_call | solution.py:587
  68.7 1.3 %write.1 = (f32[2,256,256]{2,1,0:T(8,128)}, f32[3,256,256]{2,1,0:T(8,128)}, f32[3,128,256]{2,1,0:T(8,128)}, f32[3,128,256]{2,1,0:T(8,128)}) custom-call(f32[2,256,256]{2,1,0:T(8,128)S(1)} %get-tuple-element.12.vel, f32[3,256,256]{2,1,0:T(8,128)S(1)} %get-tuple-element.13.stress, f32[256,256]{1,0:T(8,128)S(1)} %get-tuple-element.14.conc, ...), custom_call_target="tpu_custom_call" | custom-call | tf_op jit(solution)/shard_map/write/pallas_call | solution.py:623
where the time goes:
time: 70.2 us; the launch traced here: 70 us
  Pallas kernels  69.4 us (99%)
    pallas_call x1, Pallas kernels, body(): pl.pallas_call(functools.partial(step_kernel, (gx_count, gy_count, ens_co...  68 us

commit v1 on v0

--- a/solution.py
+++ b/solution.py
@@ -23,10 +23,8 @@
 
 MARGIN = SUBCYCLES
 EXTRA = 8
-TOP = 8
-LOW = TOP
-MID = TOP + MARGIN
-STEP = 16
+PAD = 8
+STEP = 32
 
 PACKED = (
     ("u", MARGIN + 1), ("v", MARGIN + 1), ("plus", MARGIN), ("minus", MARGIN), ("twice", MARGIN),
@@ -43,14 +41,14 @@
 HALF = LANES // 2
 
 OWN = 36
-AT_LEFT = MARGIN
-AT_RIGHT = MARGIN + OWN
-AT_HALO = MARGIN + 2 * OWN
-AT_END = AT_HALO + MARGIN + 1
+AT_RIGHT = 48
+AT_HALO = AT_RIGHT + OWN
+AT_LEFT = LANES - MARGIN
 
 MAIN_FIELDS = (
     "u", "v", "plus", "minus", "twice", "pressure", "inertia", "turning",
-    "ge", "gn", "ce", "cn", "cae", "can", "active",
+    "ge", "gn", "ce", "cn", "cae", "can", "bound",
+    "add", "sub", "sub_s", "add_next", "sub_next", "shear_next", "e_near", "n_near", "e_back", "n_back",
 )
 
 
@@ -67,16 +65,20 @@
     gx_count, gy_count, ens_count = sizes
     inputs, refs = refs[:9], refs[9:]
     (vel_out, stress_out, conc_out, landing), refs = refs[:4], refs[4:]
+    arrays, refs = refs[: len(MAIN_FIELDS)], refs[len(MAIN_FIELDS) :]
     (svel, sstress, sthick, sconc, smass, swind, scur, smask, sice, expand), refs = refs[:10], refs[10:]
-    arrays, refs = refs[: len(MAIN_FIELDS)], refs[len(MAIN_FIELDS) :]
     (out_a, out_b, in_a, in_b, load_sem, send_y, recv_y, send_x, recv_x, send_d, recv_d, send_e, recv_e) = refs
     field = dict(zip(MAIN_FIELDS, arrays))
     stages = (svel, sstress, sthick, sconc, smass, swind, scur, smask)
     rows, cols = conc_out.shape
     main = cols // LANES
     tiles = main + 1
-    high = MID + rows
     blocks = rows // BLOCK
+    half_rows = rows // 2
+    reach = half_rows + 2 * MARGIN
+    bases = (PAD, 3 * PAD + reach)
+    first_rows = (-MARGIN, half_rows - MARGIN)
+    spare = 5 * PAD + 2 * reach
     gx, gy, me = lax.axis_index("gx"), lax.axis_index("gy"), lax.axis_index("ens")
     right, left = lax.rem(gx + 1, gx_count), lax.rem(gx + gx_count - 1, gx_count)
     has_lo, has_hi = gy > 0, gy < gy_count - 1
@@ -167,16 +169,15 @@
         expand[8 * part * blocks : 8 * (part + 1) * blocks] = jnp.dot(
             flags, spread, preferred_element_type=jnp.float32)
 
-    def convert(start, count, ice_row):
+    def convert(start, count, ice_row, target):
         at = pl.ds(start, count)
-        to = pl.ds(start + TOP, count)
+        to = pl.ds(target, count)
         row = lax.broadcasted_iota(jnp.int32, (count, LANES), 0) + (gy * rows + (start - MARGIN))
         coriolis = CORIOLIS_TOP * (row.astype(jnp.float32) + 0.5) / (rows * gy_count)
         for t in range(main):
             c = slice(t * LANES, (t + 1) * LANES)
             present = jnp.concatenate([expand[pl.ds(ice_row, 8), c]] * (count // 8))
             alive = smask[at, c].astype(jnp.float32) * present
-            field["active"][t, to] = alive
             field["u"][t, to] = svel[0, at, c] * alive
             field["v"][t, to] = svel[1, at, c] * alive
             one, two = sstress[0, at, c], sstress[1, at, c]
@@ -191,6 +192,7 @@
             ce, cn = scur[0, at, c], scur[1, at, c]
             field["inertia"][t, to] = heavy / TIME_STEP
             field["turning"][t, to] = turn
+            field["bound"][t, to] = jnp.where(alive == 0.0, jnp.inf, turn * turn)
             field["ge"][t, to] = swind[0, at, c] + turn * cn
             field["gn"][t, to] = swind[1, at, c] - turn * ce
             field["ce"][t, to] = ce
@@ -200,15 +202,23 @@
 
     expand_ice(1)
 
-    def convert_own(block, _):
-        convert(pl.multiple_of(MARGIN + block * BLOCK, 8), BLOCK, pl.multiple_of(8 * (blocks + block), 8))
-        return 0
-
-    lax.fori_loop(0, blocks, convert_own, 0)
+    own_at = (PAD + MARGIN, bases[1] + MARGIN)
+    for half in range(2):
+        def convert_own(block, _, half=half):
+            start = pl.multiple_of(half * half_rows + block * BLOCK, 8)
+            convert(
+                MARGIN + start, BLOCK, pl.multiple_of(8 * (blocks + half * blocks // 2 + block), 8),
+                pl.multiple_of(own_at[half] + block * BLOCK, 8),
+            )
+            return 0
+
+        lax.fori_loop(0, blocks // 2, convert_own, 0)
+    convert(MARGIN + half_rows, MARGIN, 8 * (blocks + blocks // 2), own_at[0] + half_rows)
+    convert(half_rows, MARGIN, 8 * (blocks + blocks // 2 - 1), bases[1])
 
     def message(name, tile, at):
         value = field[name][tile, at]
-        return value * field["active"][tile, at] if name == "inertia" else value
+        return jnp.where(field["bound"][tile, at] == jnp.inf, 0.0, value) if name == "inertia" else value
 
     def packed(fields, at, count):
         lanes = lane_index(count)
@@ -224,19 +234,21 @@
 
     whole, part = range(WHOLE), range(WHOLE, len(PACKED))
 
-    def pack_own(block, _):
-        start = pl.multiple_of(block * BLOCK, 8)
-        east, west = packed(whole, pl.ds(MID + start, BLOCK), BLOCK)
-        out_a[0, pl.ds(start, BLOCK)] = east
-        out_a[1, pl.ds(start, BLOCK)] = west
-        return 0
-
-    lax.fori_loop(0, blocks, pack_own, 0)
+    for half in range(2):
+        def pack_own(block, _, half=half):
+            start = pl.multiple_of(block * BLOCK, 8)
+            east, west = packed(whole, pl.ds(own_at[half] + start, BLOCK), BLOCK)
+            to = pl.ds(half * half_rows + start, BLOCK)
+            out_a[0, to] = east
+            out_a[1, to] = west
+            return 0
+
+        lax.fori_loop(0, blocks // 2, pack_own, 0)
 
     def pack_half(block, _):
         start = pl.multiple_of(block * BLOCK, 8)
-        east, west = packed(part, pl.ds(MID + start, BLOCK), BLOCK)
-        more_east, more_west = packed(part, pl.ds(MID + rows // 2 + start, BLOCK), BLOCK)
+        east, west = packed(part, pl.ds(own_at[0] + start, BLOCK), BLOCK)
+        more_east, more_west = packed(part, pl.ds(own_at[1] + start, BLOCK), BLOCK)
         second = lane_index(BLOCK) >= HALF
         out_b[0, pl.ds(start, BLOCK)] = jnp.where(second, rolled(more_east, HALF), east)
         out_b[1, pl.ds(start, BLOCK)] = jnp.where(second, rolled(more_west, HALF), west)
@@ -246,7 +258,6 @@
 
     sides = (right, left)
     across, corner_lo, corner_hi = [], [], []
-    half_rows = rows // 2
     for side, to in enumerate(sides):
         across.append(remote(
             out_a.at[side], in_a.at[side, MARGIN : MARGIN + rows], send_x, recv_x, 2 * side, {"gx": to}))
@@ -280,6 +291,22 @@
         for each in corner_hi:
             each.start()
 
+    def strip_columns(target, count):
+        at = pl.ds(target, count)
+        lanes = lane_index(count)
+        for name, _ in PACKED:
+            field[name][main, at] = jnp.where(
+                lanes < OWN, message(name, 0, at), rolled(message(name, main - 1, at), AT_HALO - LANES))
+
+    for half in range(2):
+        def own_columns(block, _, half=half):
+            strip_columns(pl.multiple_of(own_at[half] + block * BLOCK, 8), BLOCK)
+            return 0
+
+        lax.fori_loop(0, blocks // 2, own_columns, 0)
+    strip_columns(own_at[0] + half_rows, MARGIN)
+    strip_columns(bases[1], MARGIN)
+
     @pl.when(has_lo)
     def _():
         for each in up:
@@ -309,10 +336,11 @@
 
     expand_ice(0)
     expand_ice(2)
-    convert(0, MARGIN, 8 * (blocks - 1))
-    convert(MARGIN + rows, MARGIN, 16 * blocks)
+    convert(0, MARGIN, 8 * (blocks - 1), bases[0])
+    convert(MARGIN + rows, MARGIN, 16 * blocks, own_at[1] + half_rows)
     beyond = slice(2 * MARGIN + rows, 2 * MARGIN + rows + EXTRA)
-    past = slice(high + MARGIN, high + MARGIN + EXTRA)
+    past = slice(bases[1] + reach, bases[1] + reach + EXTRA)
+    other_past = slice(bases[0] + reach, bases[0] + reach + EXTRA)
     for t in range(main):
         c = slice(t * LANES, (t + 1) * LANES)
         alive = smask[beyond, c].astype(jnp.float32) * expand[16 * blocks : 16 * blocks + 8, c]
@@ -344,71 +372,79 @@
             in_a[side, MARGIN + rows :] = jnp.zeros((MARGIN + EXTRA, LANES), jnp.float32)
             in_b[side, MARGIN + half_rows :] = jnp.zeros((MARGIN, LANES), jnp.float32)
 
-    def strip_value(number, start, count, half_start, half_lane):
+    def strip_value(number, row, target, count, half_start, half_lane):
         name, width = PACKED[number]
         lanes = lane_index(count)
-        at = pl.ds(start, count)
         if number < WHOLE:
-            arrived, there, lane = in_a, pl.ds(start - TOP, count), OFFSETS[number]
+            arrived, there, lane = in_a, pl.ds(row + MARGIN, count), OFFSETS[number]
         else:
             arrived, there, lane = in_b, pl.ds(half_start, count), OFFSETS[number] + half_lane
-        value = jnp.where(lanes < AT_HALO, rolled(message(name, main - 1, at), AT_HALO - LANES),
-                          rolled(arrived[1, there], AT_HALO - lane))
-        value = jnp.where(lanes < AT_RIGHT, rolled(message(name, 0, at), AT_LEFT), value)
-        value = jnp.where(lanes < AT_LEFT, rolled(arrived[0, there], -lane), value)
-        return jnp.where(lanes < AT_HALO + width, value, 0.0)
-
-    def strip_rows(start, count, half_start, half_lane):
-        at = pl.ds(start, count)
+        value = jnp.where(lanes < AT_HALO + width, rolled(arrived[1, there], AT_HALO - lane), 0.0)
+        value = jnp.where(lanes < AT_HALO, field[name][main, pl.ds(target, count)], value)
+        return jnp.where(lanes >= AT_LEFT, rolled(arrived[0, there], AT_LEFT - lane), value)
+
+    def strip_rows(first, target, count, half_start, half_lane):
+        at = pl.ds(target, count)
         value = {
-            name: strip_value(number, start, count, half_start, half_lane)
+            name: strip_value(number, first, target, count, half_start, half_lane)
             for number, (name, _) in enumerate(PACKED)
         }
-        row = lax.broadcasted_iota(jnp.int32, (count, LANES), 0) + (gy * rows + (start - MID))
+        row = lax.broadcasted_iota(jnp.int32, (count, LANES), 0) + (gy * rows + first)
         coriolis = CORIOLIS_TOP * (row.astype(jnp.float32) + 0.5) / (rows * gy_count)
         empty = value["inertia"] == 0.0
         alive = jnp.where(empty, 0.0, 1.0)
         heavy = jnp.where(empty, 1.0 / TIME_STEP, value["inertia"])
         value["inertia"] = heavy
         value["turning"] = coriolis * (heavy * TIME_STEP)
-        value["active"] = alive
+        value["bound"] = jnp.where(empty, jnp.inf, value["turning"] * value["turning"])
         value["cae"] = alive * value["ce"]
         value["can"] = alive * value["cn"]
-        for name in MAIN_FIELDS:
-            field[name][main, at] = value[name]
+        for name, each in value.items():
+            field[name][main, at] = each
 
     for half in range(2):
         def strip_own(block, _, half=half):
             start = pl.multiple_of(block * BLOCK, 8)
-            strip_rows(MID + half * half_rows + start, BLOCK, MARGIN + start, half * HALF)
+            strip_rows(half * half_rows + start, pl.multiple_of(own_at[half] + start, 8), BLOCK,
+                       MARGIN + start, half * HALF)
             return 0
 
         lax.fori_loop(0, blocks // 2, strip_own, 0)
-    strip_rows(LOW, MARGIN, 0, HALF)
-    strip_rows(high, MARGIN, MARGIN + half_rows, 0)
+    strip_rows(half_rows, own_at[0] + half_rows, MARGIN, MARGIN, HALF)
+    strip_rows(half_rows - MARGIN, bases[1], MARGIN, half_rows, 0)
+    strip_columns(bases[0], MARGIN)
+    strip_columns(own_at[1] + half_rows, MARGIN)
+    strip_rows(-MARGIN, bases[0], MARGIN, 0, HALF)
+    strip_rows(rows, own_at[1] + half_rows, MARGIN, MARGIN + half_rows, 0)
     for number in range(2):
-        field[PACKED[number][0]][main, past] = strip_value(number, high + MARGIN, EXTRA, 0, 0)
+        name = PACKED[number][0]
+        lanes = lane_index(EXTRA)
+        field[name][main, past] = jnp.where(
+            lanes < OWN, field[name][0, past], rolled(field[name][main - 1, past], AT_HALO - LANES))
+        field[name][main, past] = strip_value(number, rows + MARGIN, past.start, EXTRA, 0, 0)
+        for t in range(tiles):
+            field[name][t, other_past] = field[name][t, bases[1] + 2 * MARGIN : bases[1] + 2 * MARGIN + EXTRA]
     for name in ("plus", "minus", "twice"):
         for t in range(tiles):
-            field[name][t, 0:LOW] = jnp.zeros((LOW, LANES), jnp.float32)
+            for base in bases:
+                field[name][t, base - PAD : base] = jnp.zeros((PAD, LANES), jnp.float32)
 
     u, v, plus, minus, twice = (field[name] for name in ("u", "v", "plus", "minus", "twice"))
-    lanes = lane_index(STEP)
-    at_end, at_start = lanes == LANES - 1, lanes == 0
-
     def ahead(values):
         turned = [rolled(value, -1) for value in values]
+        at_end = lane_index(values[0].shape[0]) == LANES - 1
         return [jnp.where(at_end, turned[(t + 1) % main], turned[t]) for t in range(main)] + turned[main:]
 
     def behind(values):
         turned = [rolled(value, 1) for value in values]
+        at_start = lane_index(values[0].shape[0]) == 0
         return [jnp.where(at_start, turned[t - 1 if t else main - 1], turned[t]) for t in range(main)] + turned[main:]
 
-    def gradients(start):
+    def gradients(start, count):
         add, sub, add_s, sub_s = [], [], [], []
+        at, after = pl.ds(start, count), pl.ds(start + 1, count)
         for t in range(tiles):
-            u0, u1 = u[t, pl.ds(start, STEP)], u[t, pl.ds(start + 1, STEP)]
-            v0, v1 = v[t, pl.ds(start, STEP)], v[t, pl.ds(start + 1, STEP)]
+            u0, u1, v0, v1 = u[t, at], u[t, after], v[t, at], v[t, after]
             a, b, c, d = u0 + u1, u1 - u0, v0 + v1, v1 - v0
             add.append(a + d)
             sub.append(a - d)
@@ -416,27 +452,7 @@
             sub_s.append(b - c)
         return add, sub, add_s, sub_s
 
-    def stress_rows(start, growth):
-        at = pl.ds(start, STEP)
-        add, sub, add_s, sub_s = gradients(start)
-        add_next, sub_next, shear_next = ahead(add), ahead(sub), ahead(add_s)
-        for t in range(tiles):
-            div = add_next[t] - sub[t]
-            tension = sub_next[t] - add[t]
-            shear = shear_next[t] + sub_s[t]
-            square = div * div + (1.0 / ECCENTRICITY_SQUARED) * (tension * tension + shear * shear)
-            inverse = lax.rsqrt(jnp.maximum(square, TINY))
-            ratio = jnp.minimum(square * inverse, 1.0)
-            force = field["pressure"][t, at] * growth
-            weight = force * jnp.minimum(inverse, 1.0)
-            quarter = weight * (1.0 / ECCENTRICITY_SQUARED)
-            change = weight * div - force * ratio
-            other = quarter * tension
-            plus[t, at] = plus[t, at] + (change + other)
-            minus[t, at] = minus[t, at] + (change - other)
-            twice[t, at] = twice[t, at] + quarter * shear
-
-    def velocity_rows(start, scale):
+    def stress_sums(start):
         at, before = pl.ds(start, STEP), pl.ds(start - 1, STEP)
         e_near, e_far, n_near, n_far = [], [], [], []
         for t in range(tiles):
@@ -448,53 +464,96 @@
             e_far.append(a - d)
             n_near.append(b + e)
             n_far.append(b - e)
-        e_far, n_far = behind(e_far), behind(n_far)
+        return e_near, e_far, n_near, n_far
+
+    def stress_rows(start, growth):
+        at = pl.ds(start, STEP)
+        for t in range(tiles):
+            div = field["add_next"][t, at] - field["sub"][t, at]
+            tension = field["sub_next"][t, at] - field["add"][t, at]
+            shear = field["shear_next"][t, at] + field["sub_s"][t, at]
+            square = div * div + (1.0 / ECCENTRICITY_SQUARED) * (tension * tension + shear * shear)
+            inverse = lax.rsqrt(jnp.maximum(square, TINY))
+            weight = (field["pressure"][t, at] * growth) * jnp.minimum(inverse, 1.0)
+            quarter = weight * (1.0 / ECCENTRICITY_SQUARED)
+            change = weight * (div - square * inverse)
+            other = quarter * tension
+            plus[t, at] = plus[t, at] + (change + other)
+            minus[t, at] = minus[t, at] + (change - other)
+            twice[t, at] = twice[t, at] + quarter * shear
+
+    def velocity_rows(start, scale):
+        at = pl.ds(start, STEP)
         for t in range(tiles):
             de, dn = u[t, at] - field["ce"][t, at], v[t, at] - field["cn"][t, at]
             square = de * de + dn * dn
             drag = square * lax.rsqrt(jnp.maximum(square, TINY))
             heavy, turn = field["inertia"][t, at], field["turning"][t, at]
             diag = heavy + drag
-            push_e = heavy * de + ((e_near[t] - e_far[t]) * scale + field["ge"][t, at])
-            push_n = heavy * dn + ((n_near[t] - n_far[t]) * scale + field["gn"][t, at])
-            inverse = lax.rsqrt(diag * diag + turn * turn)
-            inverse = field["active"][t, at] * (inverse * inverse)
+            force_e = (field["e_near"][t, at] - field["e_back"][t, at]) * scale
+            force_n = (field["n_near"][t, at] - field["n_back"][t, at]) * scale
+            push_e = heavy * de + (force_e + field["ge"][t, at])
+            push_n = heavy * dn + (force_n + field["gn"][t, at])
+            inverse = lax.rsqrt(diag * diag + field["bound"][t, at])
+            inverse = inverse * inverse
             u[t, at] = (diag * push_e + turn * push_n) * inverse + field["cae"][t, at]
             v[t, at] = (diag * push_n - turn * push_e) * inverse + field["can"][t, at]
 
-    count = (high + MARGIN - LOW) // STEP
-
-    def subcycle(_, carried):
-        growth, scale = carried
-        stress_rows(LOW, growth)
-
-        def both(block, _):
-            start = pl.multiple_of(LOW + block * STEP, 8)
-            stress_rows(start, growth)
-            velocity_rows(start - STEP, scale)
-            return 0
-
-        lax.fori_loop(1, count, both, 0)
-        velocity_rows(LOW + (count - 1) * STEP, scale)
-        return growth * GAIN, scale * (1.0 / GAIN)
-
-    lax.fori_loop(0, SUBCYCLES, subcycle, (jnp.float32(GAIN), jnp.float32(0.25 / GAIN)))
+    def advance(base):
+        last = base + reach - STEP
+
+        def step(_, carried):
+            at_g, at_s, at_f, at_v, growth, growth_s, scale, scale_s, scale_f, scale_v = carried
+            at_g, at_s, at_f, at_v = (pl.multiple_of(each, 8) for each in (at_g, at_s, at_f, at_v))
+
+            def keep(names, values, start):
+                for name, each in zip(names, values):
+                    for t in range(tiles):
+                        field[name][t, pl.ds(start, STEP)] = each[t]
+
+            add, sub, add_s, sub_s = gradients(at_g, STEP)
+            add_next, sub_next, shear_next = ahead(add), ahead(sub), ahead(add_s)
+            e_near, e_far, n_near, n_far = stress_sums(at_f)
+            e_back, n_back = behind(e_far), behind(n_far)
+            stress_rows(at_s, growth_s)
+            velocity_rows(at_v, scale_v)
+            keep(("add", "sub", "sub_s", "add_next", "sub_next", "shear_next"),
+                 (add, sub, sub_s, add_next, sub_next, shear_next), at_g)
+            keep(("e_near", "n_near", "e_back", "n_back"), (e_near, n_near, e_back, n_back), at_f)
+            wrap = at_g == last
+            return (
+                jnp.where(wrap, base, jnp.where(at_g == spare, spare, at_g + STEP)), at_g, at_s, at_f,
+                jnp.where(wrap, growth * GAIN, growth), growth,
+                jnp.where(wrap, scale * (1.0 / GAIN), scale), scale, scale_s, scale_f,
+            )
+
+        one = jnp.float32(1.0)
+        empty = jnp.int32(spare)
+        start = (jnp.int32(base), empty, empty, empty, one * GAIN, one, one * (0.25 / GAIN), one, one, one)
+        carried = lax.fori_loop(0, SUBCYCLES * (reach // STEP), step, start)
+        lax.fori_loop(0, 3, step, (empty,) + carried[1:])
 
     shrink = 0.5 * GAIN**-SUBCYCLES
-    on_left, on_right = lanes < MARGIN, lanes >= LANES - MARGIN - 2
 
     def merged(values):
+        lanes = lane_index(values[0].shape[0])
+        on_left, on_right = lanes < MARGIN, lanes >= LANES - MARGIN - 2
         values = list(values)
-        values[0] = jnp.where(on_left, rolled(values[main], -AT_LEFT), values[0])
+        values[0] = jnp.where(on_left, values[main], values[0])
         values[main - 1] = jnp.where(on_right, rolled(values[main], LANES - AT_HALO), values[main - 1])
         return values[:main]
 
-    def finish(block, _):
-        start = pl.multiple_of(block * STEP, 8)
-        here, at = pl.ds(MID + start, STEP), pl.ds(start, STEP)
-        add, sub, _, _ = gradients(MID + start)
+    def finish_conc(start, row, count):
+        add, sub, _, _ = gradients(start, count)
         add_next = ahead(add)
         div = merged([add_next[t] - sub[t] for t in range(tiles)])
+        for t in range(main):
+            c = slice(t * LANES, (t + 1) * LANES)
+            value = sconc[pl.ds(MARGIN + row, count), c]
+            conc_out[pl.ds(row, count), c] = jnp.clip(value - value * (0.5 * div[t]), 0.0, 1.0)
+
+    def finish(start, row, count):
+        here, at = pl.ds(start, count), pl.ds(row, count)
         east, north, one, two, three = (
             merged([ref[t, here] for t in range(tiles)]) for ref in (u, v, plus, minus, twice)
         )
@@ -505,22 +564,40 @@
             stress_out[0, at, c] = (one[t] + two[t]) * shrink
             stress_out[1, at, c] = (one[t] - two[t]) * shrink
             stress_out[2, at, c] = three[t] * shrink
-            value = sconc[pl.ds(MARGIN + start, STEP), c]
-            conc_out[at, c] = jnp.clip(value - value * (0.5 * div[t]), 0.0, 1.0)
-        return 0
-
-    lax.fori_loop(0, rows // STEP, finish, 0)
-
+        finish_conc(start, row, count)
+
+    def finish_half(half):
+        def body(block, _):
+            start = block * BLOCK
+            finish(
+                pl.multiple_of(jnp.where(half == 0, own_at[0], own_at[1]) + start, 8),
+                pl.multiple_of(half * half_rows + start, 8), BLOCK,
+            )
+            return 0
+
+        lax.fori_loop(0, half_rows // BLOCK, body, 0)
+
+    early = (1 - me) if ens_count == 2 else jnp.int32(0)
+    late = 1 - early
     share = rows // ens_count
     swaps = []
     for step, peer in enumerate(peers):
         part_of = pl.ds(pl.multiple_of(peer * share, 8), share)
         swaps.append(remote(
-            conc_out.at[part_of], landing.at[step, 0], send_e, recv_e, 2 * step, {"ens": peer}))
+            vel_out.at[:, part_of], landing.at[step, 1:3], send_e, recv_e, 2 * step, {"ens": peer}))
         swaps.append(remote(
-            vel_out.at[:, part_of], landing.at[step, 1:3], send_e, recv_e, 2 * step + 1, {"ens": peer}))
-    for each in swaps:
-        each.start()
+            conc_out.at[part_of], landing.at[step, 0], send_e, recv_e, 2 * step + 1, {"ens": peer}))
+
+    advance(jnp.where(early == 0, bases[0], bases[1]))
+    finish_half(early)
+    if ens_count == 2:
+        for each in swaps:
+            each.start()
+    advance(jnp.where(late == 0, bases[0], bases[1]))
+    finish_half(late)
+    if ens_count != 2:
+        for each in swaps:
+            each.start()
     for each in across:
         each.wait_send()
 
@@ -581,7 +658,7 @@
         tiles = cols // LANES + 1
         block_rows, block_cols = ice.shape[1:]
         tall = rows + 2 * MARGIN
-        total = TOP + tall + EXTRA
+        total = -(-(5 * PAD + 2 * (rows // 2 + 2 * MARGIN) + STEP + PAD) // 32) * 32
         shape = lambda *dims: jax.ShapeDtypeStruct(dims, f32)
         dma = lambda count: pltpu.SemaphoreType.DMA((count,))
         state = pl.pallas_call(
@@ -595,7 +672,8 @@
             ),
             in_specs=specs(9, pltpu.HBM),
             out_specs=tuple(specs(4, pltpu.VMEM)),
-            scratch_shapes=[
+            scratch_shapes=[vmem(tiles, total, LANES)] * len(MAIN_FIELDS)
+            + [
                 vmem(2, tall + EXTRA, cols),
                 vmem(3, tall, cols),
                 vmem(tall, cols),
@@ -606,9 +684,6 @@
                 vmem(tall + EXTRA, cols, dtype=jnp.int32),
                 vmem(3 * block_rows, block_cols, dtype=jnp.int32),
                 vmem(24 * block_rows, cols),
-            ]
-            + [vmem(tiles, total, LANES)] * len(MAIN_FIELDS)
-            + [
                 vmem(2, rows, LANES),
                 vmem(2, rows // 2, LANES),
                 vmem(2, tall + EXTRA, LANES),
@@ -617,7 +692,7 @@
                 dma(2 * (ens_count - 1)), dma(2 * (ens_count - 1)),
             ],
             compiler_params=pltpu.CompilerParams(
-                collective_id=0, has_side_effects=True, vmem_limit_bytes=24 << 20),
+                collective_id=0, has_side_effects=True, vmem_limit_bytes=28 << 20),
         )(*(pltpu.with_memory_space_constraint(each, pltpu.HBM) for each in (
             velocity[0], stress[0], thickness[0], concentration[0], node_mass[0], wind[0], current[0], mask, ice[0])))
         vel_out, stress_out, mean, spread = pl.pallas_call(

time: 70.2 us -> 46.9 us (0.67)
  Pallas kernels: 69.4 us -> 46.1 us
    pallas_call x1, Pallas kernels: 68 us -> 44.7 us  [body(): pl.pallas_call(functools.partial(step_kernel, (gx_count, gy_count, ens_co...]
where the time goes in v1:
time: 46.9 us; the launch traced here: 46.7 us
  Pallas kernels  46.1 us (98%)
  between operations  0.64 us (1%)
    pallas_call x1, Pallas kernels, body(): pl.pallas_call(functools.partial(step_kernel, (gx_count, gy_count, ens_co...  44.7 us
    pallas_call x1, Pallas kernels, body(): pl.pallas_call(functools.partial(write_kernel, ens_count), name='write',...  1.34 us

profile of v1, /device:TPU:0, one launch (start us, length us, event | category | flops | bytes accessed | tf_op | source)
XLA Modules:
  0.0 46.7 jit_solution(7860499635115864663)
XLA Ops:
  0.6 44.7 %subcycles.1 = (f32[2,256,256]{2,1,0:T(8,128)S(1)}, f32[3,256,256]{2,1,0:T(8,128)S(1)}, f32[256,256]{1,0:T(8,128)S(1)}, f32[1,3,128,256]{3,2,1,0:T(8,128)S(1)}) custom-call(f32[2,256,256]{2,1,0:T(8,128)} %bitcast.11, f32[3,256,256]{2,1,0:T(8,128)} %bitcast.10, f32[256,256]{1,0:T(8,128)} %bitcast.14, f32[256,256]{1,0:T(8,128)} %bitcast.15, ...), custom_call_target="tpu_custom_call" | custom-call | tf_op jit(solution)/shard_map/subcycles/pallas_call | solution.py:664
  45.4 1.3 %write.1 = (f32[2,256,256]{2,1,0:T(8,128)}, f32[3,256,256]{2,1,0:T(8,128)}, f32[3,128,256]{2,1,0:T(8,128)}, f32[3,128,256]{2,1,0:T(8,128)}) custom-call(f32[2,256,256]{2,1,0:T(8,128)S(1)} %get-tuple-element.12.vel, f32[3,256,256]{2,1,0:T(8,128)S(1)} %get-tuple-element.13.stress, f32[256,256]{1,0:T(8,128)S(1)} %get-tuple-element.14.conc, ...), custom_call_target="tpu_custom_call" | custom-call | tf_op jit(solution)/shard_map/write/pallas_call | solution.py:698

commit v2 on v1

--- a/solution.py
+++ b/solution.py
@@ -24,6 +24,7 @@
 MARGIN = SUBCYCLES
 EXTRA = 8
 PAD = 8
+CHUNK = 64
 STEP = 32
 
 PACKED = (
@@ -47,8 +48,8 @@
 
 MAIN_FIELDS = (
     "u", "v", "plus", "minus", "twice", "pressure", "inertia", "turning",
-    "ge", "gn", "ce", "cn", "cae", "can", "bound",
-    "add", "sub", "sub_s", "add_next", "sub_next", "shear_next", "e_near", "n_near", "e_back", "n_back",
+    "ge", "gn", "ce", "cn", "bound",
+    "u_next", "v_next", "e_near", "n_near", "e_back", "n_back",
 )
 
 
@@ -101,17 +102,19 @@
             greet(gy=row, gx=left)
             greet(gy=row, gx=right)
 
-    own = slice(MARGIN, MARGIN + rows)
-
     def at_rows(ref, where):
         return ref.at[:, where] if len(ref.shape) == 3 else ref.at[where]
 
-    loads = [
-        pltpu.make_async_copy(source, at_rows(stage, own), load_sem.at[number])
+    loads = [[
+        pltpu.make_async_copy(
+            at_rows(source, slice(half * half_rows, (half + 1) * half_rows)),
+            at_rows(stage, slice(MARGIN + half * half_rows, MARGIN + (half + 1) * half_rows)),
+            load_sem.at[8 * half + number],
+        )
         for number, (source, stage) in enumerate(zip(inputs, stages))
-    ]
-    loads.append(pltpu.make_async_copy(inputs[8], sice.at[blocks : 2 * blocks], load_sem.at[8]))
-    for each in loads:
+    ] for half in range(2)]
+    loads[0].append(pltpu.make_async_copy(inputs[8], sice.at[blocks : 2 * blocks], load_sem.at[16]))
+    for each in loads[0] + loads[1]:
         each.start()
 
     def remote(source, target, sends, receives, number, where):
@@ -149,9 +152,6 @@
         for each in up:
             each.start()
 
-    for each in loads:
-        each.wait()
-
     block_cols = sice.shape[1]
     spread = (
         lax.broadcasted_iota(jnp.int32, (block_cols, cols), 1) // BLOCK
@@ -174,87 +174,75 @@
         to = pl.ds(target, count)
         row = lax.broadcasted_iota(jnp.int32, (count, LANES), 0) + (gy * rows + (start - MARGIN))
         coriolis = CORIOLIS_TOP * (row.astype(jnp.float32) + 0.5) / (rows * gy_count)
+        sent = []
         for t in range(main):
             c = slice(t * LANES, (t + 1) * LANES)
             present = jnp.concatenate([expand[pl.ds(ice_row, 8), c]] * (count // 8))
             alive = smask[at, c].astype(jnp.float32) * present
-            field["u"][t, to] = svel[0, at, c] * alive
-            field["v"][t, to] = svel[1, at, c] * alive
             one, two = sstress[0, at, c], sstress[1, at, c]
-            field["plus"][t, to] = one + two
-            field["minus"][t, to] = one - two
-            field["twice"][t, to] = 2.0 * sstress[2, at, c]
             factor = RELAX_RATE * 0.5 / GAIN
-            field["pressure"][t, to] = factor * sthick[at, c] * jnp.exp(-STRENGTH_DECAY * (1.0 - sconc[at, c]))
             heavy = smass[at, c]
             heavy = jnp.where(heavy == 0.0, 1.0, heavy)
             turn = coriolis * heavy
             ce, cn = scur[0, at, c], scur[1, at, c]
-            field["inertia"][t, to] = heavy / TIME_STEP
-            field["turning"][t, to] = turn
-            field["bound"][t, to] = jnp.where(alive == 0.0, jnp.inf, turn * turn)
-            field["ge"][t, to] = swind[0, at, c] + turn * cn
-            field["gn"][t, to] = swind[1, at, c] - turn * ce
-            field["ce"][t, to] = ce
-            field["cn"][t, to] = cn
-            field["cae"][t, to] = alive * ce
-            field["can"][t, to] = alive * cn
-
-    expand_ice(1)
+            value = {
+                "u": svel[0, at, c] * alive,
+                "v": svel[1, at, c] * alive,
+                "plus": one + two,
+                "minus": one - two,
+                "twice": 2.0 * sstress[2, at, c],
+                "pressure": factor * sthick[at, c] * jnp.exp(-STRENGTH_DECAY * (1.0 - sconc[at, c])),
+                "inertia": heavy / TIME_STEP,
+                "turning": turn,
+                "bound": jnp.where(alive == 0.0, jnp.inf, turn * turn),
+                "ge": swind[0, at, c] + turn * cn,
+                "gn": swind[1, at, c] - turn * ce,
+                "ce": alive * ce,
+                "cn": alive * cn,
+            }
+            for name, each in value.items():
+                field[name][t, to] = each
+            value["inertia"] = value["inertia"] * alive
+            sent.append(value)
+        return sent
+
+    whole, part = range(WHOLE), range(WHOLE, len(PACKED))
+
+    def packed(sent, fields, shift, east, west):
+        lanes = lane_index(east.shape[0])
+        for number in fields:
+            name, width = PACKED[number]
+            start = OFFSETS[number] + shift
+            here = jnp.logical_and(lanes >= start, lanes < start + width)
+            east = jnp.where(here, rolled(sent[main - 1][name], start - (LANES - MARGIN)), east)
+            west = jnp.where(here, rolled(sent[0][name], start), west)
+        return east, west
 
     own_at = (PAD + MARGIN, bases[1] + MARGIN)
     for half in range(2):
+        for each in loads[half]:
+            each.wait()
+        if half == 0:
+            expand_ice(1)
+
         def convert_own(block, _, half=half):
             start = pl.multiple_of(half * half_rows + block * BLOCK, 8)
-            convert(
+            sent = convert(
                 MARGIN + start, BLOCK, pl.multiple_of(8 * (blocks + half * blocks // 2 + block), 8),
                 pl.multiple_of(own_at[half] + block * BLOCK, 8),
             )
+            zero = jnp.zeros((BLOCK, LANES), jnp.float32)
+            to, to_half = pl.ds(start, BLOCK), pl.ds(pl.multiple_of(block * BLOCK, 8), BLOCK)
+            out_a[0, to], out_a[1, to] = packed(sent, whole, 0, zero, zero)
+            before = (out_b[0, to_half], out_b[1, to_half]) if half else (zero, zero)
+            out_b[0, to_half], out_b[1, to_half] = packed(sent, part, half * HALF, *before)
             return 0
 
         lax.fori_loop(0, blocks // 2, convert_own, 0)
-    convert(MARGIN + half_rows, MARGIN, 8 * (blocks + blocks // 2), own_at[0] + half_rows)
-    convert(half_rows, MARGIN, 8 * (blocks + blocks // 2 - 1), bases[1])
 
     def message(name, tile, at):
         value = field[name][tile, at]
         return jnp.where(field["bound"][tile, at] == jnp.inf, 0.0, value) if name == "inertia" else value
-
-    def packed(fields, at, count):
-        lanes = lane_index(count)
-        east = jnp.zeros((count, LANES), jnp.float32)
-        west = jnp.zeros((count, LANES), jnp.float32)
-        for number in fields:
-            name, width = PACKED[number]
-            start = OFFSETS[number]
-            here = jnp.logical_and(lanes >= start, lanes < start + width)
-            east = jnp.where(here, rolled(message(name, main - 1, at), start - (LANES - MARGIN)), east)
-            west = jnp.where(here, rolled(message(name, 0, at), start), west)
-        return east, west
-
-    whole, part = range(WHOLE), range(WHOLE, len(PACKED))
-
-    for half in range(2):
-        def pack_own(block, _, half=half):
-            start = pl.multiple_of(block * BLOCK, 8)
-            east, west = packed(whole, pl.ds(own_at[half] + start, BLOCK), BLOCK)
-            to = pl.ds(half * half_rows + start, BLOCK)
-            out_a[0, to] = east
-            out_a[1, to] = west
-            return 0
-
-        lax.fori_loop(0, blocks // 2, pack_own, 0)
-
-    def pack_half(block, _):
-        start = pl.multiple_of(block * BLOCK, 8)
-        east, west = packed(part, pl.ds(own_at[0] + start, BLOCK), BLOCK)
-        more_east, more_west = packed(part, pl.ds(own_at[1] + start, BLOCK), BLOCK)
-        second = lane_index(BLOCK) >= HALF
-        out_b[0, pl.ds(start, BLOCK)] = jnp.where(second, rolled(more_east, HALF), east)
-        out_b[1, pl.ds(start, BLOCK)] = jnp.where(second, rolled(more_west, HALF), west)
-        return 0
-
-    lax.fori_loop(0, blocks // 2, pack_half, 0)
 
     sides = (right, left)
     across, corner_lo, corner_hi = [], [], []
@@ -291,6 +279,9 @@
         for each in corner_hi:
             each.start()
 
+    convert(MARGIN + half_rows, MARGIN, 8 * (blocks + blocks // 2), own_at[0] + half_rows)
+    convert(half_rows, MARGIN, 8 * (blocks + blocks // 2 - 1), bases[1])
+
     def strip_columns(target, count):
         at = pl.ds(target, count)
         lanes = lane_index(count)
@@ -300,10 +291,10 @@
 
     for half in range(2):
         def own_columns(block, _, half=half):
-            strip_columns(pl.multiple_of(own_at[half] + block * BLOCK, 8), BLOCK)
+            strip_columns(pl.multiple_of(own_at[half] + block * CHUNK, 8), CHUNK)
             return 0
 
-        lax.fori_loop(0, blocks // 2, own_columns, 0)
+        lax.fori_loop(0, half_rows // CHUNK, own_columns, 0)
     strip_columns(own_at[0] + half_rows, MARGIN)
     strip_columns(bases[1], MARGIN)
 
@@ -392,24 +383,21 @@
         row = lax.broadcasted_iota(jnp.int32, (count, LANES), 0) + (gy * rows + first)
         coriolis = CORIOLIS_TOP * (row.astype(jnp.float32) + 0.5) / (rows * gy_count)
         empty = value["inertia"] == 0.0
-        alive = jnp.where(empty, 0.0, 1.0)
         heavy = jnp.where(empty, 1.0 / TIME_STEP, value["inertia"])
         value["inertia"] = heavy
         value["turning"] = coriolis * (heavy * TIME_STEP)
         value["bound"] = jnp.where(empty, jnp.inf, value["turning"] * value["turning"])
-        value["cae"] = alive * value["ce"]
-        value["can"] = alive * value["cn"]
         for name, each in value.items():
             field[name][main, at] = each
 
     for half in range(2):
         def strip_own(block, _, half=half):
-            start = pl.multiple_of(block * BLOCK, 8)
-            strip_rows(half * half_rows + start, pl.multiple_of(own_at[half] + start, 8), BLOCK,
+            start = pl.multiple_of(block * CHUNK, 8)
+            strip_rows(half * half_rows + start, pl.multiple_of(own_at[half] + start, 8), CHUNK,
                        MARGIN + start, half * HALF)
             return 0
 
-        lax.fori_loop(0, blocks // 2, strip_own, 0)
+        lax.fori_loop(0, half_rows // CHUNK, strip_own, 0)
     strip_rows(half_rows, own_at[0] + half_rows, MARGIN, MARGIN, HALF)
     strip_rows(half_rows - MARGIN, bases[1], MARGIN, half_rows, 0)
     strip_columns(bases[0], MARGIN)
@@ -430,6 +418,7 @@
                 field[name][t, base - PAD : base] = jnp.zeros((PAD, LANES), jnp.float32)
 
     u, v, plus, minus, twice = (field[name] for name in ("u", "v", "plus", "minus", "twice"))
+    u_next, v_next = field["u_next"], field["v_next"]
     def ahead(values):
         turned = [rolled(value, -1) for value in values]
         at_end = lane_index(values[0].shape[0]) == LANES - 1
@@ -467,11 +456,13 @@
         return e_near, e_far, n_near, n_far
 
     def stress_rows(start, growth):
-        at = pl.ds(start, STEP)
+        at, after = pl.ds(start, STEP), pl.ds(start + 1, STEP)
         for t in range(tiles):
-            div = field["add_next"][t, at] - field["sub"][t, at]
-            tension = field["sub_next"][t, at] - field["add"][t, at]
-            shear = field["shear_next"][t, at] + field["sub_s"][t, at]
+            u0, u1, v0, v1 = u[t, at], u[t, after], v[t, at], v[t, after]
+            u2, u3, v2, v3 = u_next[t, at], u_next[t, after], v_next[t, at], v_next[t, after]
+            along, across_y = (u2 + u3) - (u0 + u1), (v1 - v0) + (v3 - v2)
+            div, tension = along + across_y, along - across_y
+            shear = ((u1 - u0) + (u3 - u2)) + ((v2 + v3) - (v0 + v1))
             square = div * div + (1.0 / ECCENTRICITY_SQUARED) * (tension * tension + shear * shear)
             inverse = lax.rsqrt(jnp.maximum(square, TINY))
             weight = (field["pressure"][t, at] * growth) * jnp.minimum(inverse, 1.0)
@@ -485,7 +476,8 @@
     def velocity_rows(start, scale):
         at = pl.ds(start, STEP)
         for t in range(tiles):
-            de, dn = u[t, at] - field["ce"][t, at], v[t, at] - field["cn"][t, at]
+            ce, cn = field["ce"][t, at], field["cn"][t, at]
+            de, dn = u[t, at] - ce, v[t, at] - cn
             square = de * de + dn * dn
             drag = square * lax.rsqrt(jnp.maximum(square, TINY))
             heavy, turn = field["inertia"][t, at], field["turning"][t, at]
@@ -496,42 +488,40 @@
             push_n = heavy * dn + (force_n + field["gn"][t, at])
             inverse = lax.rsqrt(diag * diag + field["bound"][t, at])
             inverse = inverse * inverse
-            u[t, at] = (diag * push_e + turn * push_n) * inverse + field["cae"][t, at]
-            v[t, at] = (diag * push_n - turn * push_e) * inverse + field["can"][t, at]
-
-    def advance(base):
+            u[t, at] = (diag * push_e + turn * push_n) * inverse + ce
+            v[t, at] = (diag * push_n - turn * push_e) * inverse + cn
+
+    def run(count, base, carried):
         last = base + reach - STEP
 
         def step(_, carried):
-            at_g, at_s, at_f, at_v, growth, growth_s, scale, scale_s, scale_f, scale_v = carried
-            at_g, at_s, at_f, at_v = (pl.multiple_of(each, 8) for each in (at_g, at_s, at_f, at_v))
+            at_g, at_h, at_s, at_f, at_v, growth, growth_h, growth_s, scale, scale_h, scale_s, scale_f, scale_v = carried
+            at_g, at_h, at_s, at_f, at_v = (pl.multiple_of(each, 8) for each in (at_g, at_h, at_s, at_f, at_v))
 
             def keep(names, values, start):
                 for name, each in zip(names, values):
                     for t in range(tiles):
                         field[name][t, pl.ds(start, STEP)] = each[t]
 
-            add, sub, add_s, sub_s = gradients(at_g, STEP)
-            add_next, sub_next, shear_next = ahead(add), ahead(sub), ahead(add_s)
+            moved = [ahead([ref[t, pl.ds(at_g, STEP)] for t in range(tiles)]) for ref in (u, v)]
             e_near, e_far, n_near, n_far = stress_sums(at_f)
             e_back, n_back = behind(e_far), behind(n_far)
             stress_rows(at_s, growth_s)
             velocity_rows(at_v, scale_v)
-            keep(("add", "sub", "sub_s", "add_next", "sub_next", "shear_next"),
-                 (add, sub, sub_s, add_next, sub_next, shear_next), at_g)
+            keep(("u_next", "v_next"), moved, at_g)
             keep(("e_near", "n_near", "e_back", "n_back"), (e_near, n_near, e_back, n_back), at_f)
             wrap = at_g == last
             return (
-                jnp.where(wrap, base, jnp.where(at_g == spare, spare, at_g + STEP)), at_g, at_s, at_f,
-                jnp.where(wrap, growth * GAIN, growth), growth,
-                jnp.where(wrap, scale * (1.0 / GAIN), scale), scale, scale_s, scale_f,
+                jnp.where(wrap, base, jnp.where(at_g == spare, spare, at_g + STEP)), at_g, at_h, at_s, at_f,
+                jnp.where(wrap, growth * GAIN, growth), growth, growth_h,
+                jnp.where(wrap, scale * (1.0 / GAIN), scale), scale, scale_h, scale_s, scale_f,
             )
 
-        one = jnp.float32(1.0)
-        empty = jnp.int32(spare)
-        start = (jnp.int32(base), empty, empty, empty, one * GAIN, one, one * (0.25 / GAIN), one, one, one)
-        carried = lax.fori_loop(0, SUBCYCLES * (reach // STEP), step, start)
-        lax.fori_loop(0, 3, step, (empty,) + carried[1:])
+        return lax.fori_loop(0, count, step, carried)
+
+    def begin(at, carried):
+        growth, scale = jnp.float32(GAIN), jnp.float32(0.25 / GAIN)
+        return (jnp.int32(at),) + carried[1:5] + (growth,) + carried[6:8] + (scale,) + carried[9:]
 
     shrink = 0.5 * GAIN**-SUBCYCLES
 
@@ -568,14 +558,14 @@
 
     def finish_half(half):
         def body(block, _):
-            start = block * BLOCK
+            start = block * CHUNK
             finish(
                 pl.multiple_of(jnp.where(half == 0, own_at[0], own_at[1]) + start, 8),
-                pl.multiple_of(half * half_rows + start, 8), BLOCK,
+                pl.multiple_of(half * half_rows + start, 8), CHUNK,
             )
             return 0
 
-        lax.fori_loop(0, half_rows // BLOCK, body, 0)
+        lax.fori_loop(0, half_rows // CHUNK, body, 0)
 
     early = (1 - me) if ens_count == 2 else jnp.int32(0)
     late = 1 - early
@@ -588,12 +578,23 @@
         swaps.append(remote(
             conc_out.at[part_of], landing.at[step, 0], send_e, recv_e, 2 * step + 1, {"ens": peer}))
 
-    advance(jnp.where(early == 0, bases[0], bases[1]))
+    for beyond_domain in (past, other_past):
+        for ref, target in ((u, u_next), (v, v_next)):
+            for t, each in enumerate(ahead([ref[t, beyond_domain] for t in range(tiles)])):
+                target[t, beyond_domain] = each
+    steps, lag = SUBCYCLES * (reach // STEP), 4
+    one, empty = jnp.float32(1.0), jnp.int32(spare)
+    first = jnp.where(early == 0, bases[0], bases[1])
+    second = jnp.where(late == 0, bases[0], bases[1])
+    carried = begin(first, (empty,) * 5 + (one,) * 8)
+    carried = run(steps, first, carried)
+    carried = run(lag, second, begin(second, carried))
     finish_half(early)
     if ens_count == 2:
         for each in swaps:
             each.start()
-    advance(jnp.where(late == 0, bases[0], bases[1]))
+    carried = run(steps - lag, second, carried)
+    run(lag, spare, begin(spare, carried))
     finish_half(late)
     if ens_count != 2:
         for each in swaps:
@@ -688,7 +689,7 @@
                 vmem(2, rows // 2, LANES),
                 vmem(2, tall + EXTRA, LANES),
                 vmem(2, rows // 2 + 2 * MARGIN, LANES),
-                dma(9), dma(18), dma(18), dma(4), dma(4), dma(8), dma(8),
+                dma(17), dma(18), dma(18), dma(4), dma(4), dma(8), dma(8),
                 dma(2 * (ens_count - 1)), dma(2 * (ens_count - 1)),
             ],
             compiler_params=pltpu.CompilerParams(

time: 46.9 us -> 45.7 us (0.974)
  Pallas kernels: 46.1 us -> 44.9 us
    pallas_call x1, Pallas kernels: 44.7 us -> 43.5 us  [body(): pl.pallas_call(functools.partial(step_kernel, (gx_count, gy_count, ens_co...]
where the time goes in v2:
time: 45.7 us; the launch traced here: 45.5 us
  Pallas kernels  44.9 us (98%)
  between operations  0.64 us (1%)
    pallas_call x1, Pallas kernels, body(): pl.pallas_call(functools.partial(step_kernel, (gx_count, gy_count, ens_co...  43.5 us
    pallas_call x1, Pallas kernels, body(): pl.pallas_call(functools.partial(write_kernel, ens_count), name='write',...  1.34 us

profile of v2, /device:TPU:0, one launch (start us, length us, event | category | flops | bytes accessed | tf_op | source)
XLA Modules:
  0.0 45.5 jit_solution(9583285372916865332)
XLA Ops:
  0.6 43.5 %subcycles.1 = (f32[2,256,256]{2,1,0:T(8,128)S(1)}, f32[3,256,256]{2,1,0:T(8,128)S(1)}, f32[256,256]{1,0:T(8,128)S(1)}, f32[1,3,128,256]{3,2,1,0:T(8,128)S(1)}) custom-call(f32[2,256,256]{2,1,0:T(8,128)} %bitcast.11, f32[3,256,256]{2,1,0:T(8,128)} %bitcast.10, f32[256,256]{1,0:T(8,128)} %bitcast.14, f32[256,256]{1,0:T(8,128)} %bitcast.15, ...), custom_call_target="tpu_custom_call" | custom-call | tf_op jit(solution)/shard_map/subcycles/pallas_call | solution.py:665
  44.2 1.3 %write.1 = (f32[2,256,256]{2,1,0:T(8,128)}, f32[3,256,256]{2,1,0:T(8,128)}, f32[3,128,256]{2,1,0:T(8,128)}, f32[3,128,256]{2,1,0:T(8,128)}) custom-call(f32[2,256,256]{2,1,0:T(8,128)S(1)} %get-tuple-element.12.vel, f32[3,256,256]{2,1,0:T(8,128)S(1)} %get-tuple-element.13.stress, f32[256,256]{1,0:T(8,128)S(1)} %get-tuple-element.14.conc, ...), custom_call_target="tpu_custom_call" | custom-call | tf_op jit(solution)/shard_map/write/pallas_call | solution.py:699

commit v3 on v2

--- a/solution.py
+++ b/solution.py
@@ -48,7 +48,7 @@
 
 MAIN_FIELDS = (
     "u", "v", "plus", "minus", "twice", "pressure", "inertia", "turning",
-    "ge", "gn", "ce", "cn", "bound",
+    "ge", "gn", "ce", "cn", "bound", "re", "rn",
     "u_next", "v_next", "e_near", "n_near", "e_back", "n_back",
 )
 
@@ -200,6 +200,7 @@
                 "ce": alive * ce,
                 "cn": alive * cn,
             }
+            value["re"], value["rn"] = value["u"] - value["ce"], value["v"] - value["cn"]
             for name, each in value.items():
                 field[name][t, to] = each
             value["inertia"] = value["inertia"] * alive
@@ -387,6 +388,7 @@
         value["inertia"] = heavy
         value["turning"] = coriolis * (heavy * TIME_STEP)
         value["bound"] = jnp.where(empty, jnp.inf, value["turning"] * value["turning"])
+        value["re"], value["rn"] = value["u"] - value["ce"], value["v"] - value["cn"]
         for name, each in value.items():
             field[name][main, at] = each
 
@@ -456,8 +458,8 @@
         return e_near, e_far, n_near, n_far
 
     def stress_rows(start, growth):
-        at, after = pl.ds(start, STEP), pl.ds(start + 1, STEP)
-        for t in range(tiles):
+        for t, piece in [(t, piece) for t in range(tiles) for piece in range(0, STEP, 8)]:
+            at, after = pl.ds(start + piece, 8), pl.ds(start + piece + 1, 8)
             u0, u1, v0, v1 = u[t, at], u[t, after], v[t, at], v[t, after]
             u2, u3, v2, v3 = u_next[t, at], u_next[t, after], v_next[t, at], v_next[t, after]
             along, across_y = (u2 + u3) - (u0 + u1), (v1 - v0) + (v3 - v2)
@@ -474,10 +476,9 @@
             twice[t, at] = twice[t, at] + quarter * shear
 
     def velocity_rows(start, scale):
-        at = pl.ds(start, STEP)
-        for t in range(tiles):
-            ce, cn = field["ce"][t, at], field["cn"][t, at]
-            de, dn = u[t, at] - ce, v[t, at] - cn
+        for t, piece in [(t, piece) for t in range(tiles) for piece in range(0, STEP, 8)]:
+            at = pl.ds(start + piece, 8)
+            de, dn = field["re"][t, at], field["rn"][t, at]
             square = de * de + dn * dn
             drag = square * lax.rsqrt(jnp.maximum(square, TINY))
             heavy, turn = field["inertia"][t, at], field["turning"][t, at]
@@ -488,8 +489,11 @@
             push_n = heavy * dn + (force_n + field["gn"][t, at])
             inverse = lax.rsqrt(diag * diag + field["bound"][t, at])
             inverse = inverse * inverse
-            u[t, at] = (diag * push_e + turn * push_n) * inverse + ce
-            v[t, at] = (diag * push_n - turn * push_e) * inverse + cn
+            de = (diag * push_e + turn * push_n) * inverse
+            dn = (diag * push_n - turn * push_e) * inverse
+            field["re"][t, at], field["rn"][t, at] = de, dn
+            u[t, at] = de + field["ce"][t, at]
+            v[t, at] = dn + field["cn"][t, at]
 
     def run(count, base, carried):
         last = base + reach - STEP
@@ -693,7 +697,7 @@
                 dma(2 * (ens_count - 1)), dma(2 * (ens_count - 1)),
             ],
             compiler_params=pltpu.CompilerParams(
-                collective_id=0, has_side_effects=True, vmem_limit_bytes=28 << 20),
+                collective_id=0, has_side_effects=True, vmem_limit_bytes=32 << 20),
         )(*(pltpu.with_memory_space_constraint(each, pltpu.HBM) for each in (
             velocity[0], stress[0], thickness[0], concentration[0], node_mass[0], wind[0], current[0], mask, ice[0])))
         vel_out, stress_out, mean, spread = pl.pallas_call(

time: 45.7 us -> 45.3 us (level)
  no operation moved by 1% of the time
where the time goes in v3:
time: 45.3 us; the launch traced here: 45.2 us
  Pallas kernels  44.5 us (98%)
  between operations  0.64 us (1%)
    pallas_call x1, Pallas kernels, body(): pl.pallas_call(functools.partial(step_kernel, (gx_count, gy_count, ens_co...  43.2 us
    pallas_call x1, Pallas kernels, body(): pl.pallas_call(functools.partial(write_kernel, ens_count), name='write',...  1.34 us

profile of v3, /device:TPU:0, one launch (start us, length us, event | category | flops | bytes accessed | tf_op | source)
XLA Modules:
  0.0 45.2 jit_solution(7136584672238156462)
XLA Ops:
  0.6 43.2 %subcycles.1 = (f32[2,256,256]{2,1,0:T(8,128)S(1)}, f32[3,256,256]{2,1,0:T(8,128)S(1)}, f32[256,256]{1,0:T(8,128)S(1)}, f32[1,3,128,256]{3,2,1,0:T(8,128)S(1)}) custom-call(f32[2,256,256]{2,1,0:T(8,128)} %bitcast.11, f32[3,256,256]{2,1,0:T(8,128)} %bitcast.10, f32[256,256]{1,0:T(8,128)} %bitcast.14, f32[256,256]{1,0:T(8,128)} %bitcast.15, ...), custom_call_target="tpu_custom_call" | custom-call | tf_op jit(solution)/shard_map/subcycles/pallas_call | solution.py:669
  43.8 1.3 %write.1 = (f32[2,256,256]{2,1,0:T(8,128)}, f32[3,256,256]{2,1,0:T(8,128)}, f32[3,128,256]{2,1,0:T(8,128)}, f32[3,128,256]{2,1,0:T(8,128)}) custom-call(f32[2,256,256]{2,1,0:T(8,128)S(1)} %get-tuple-element.12.vel, f32[3,256,256]{2,1,0:T(8,128)S(1)} %get-tuple-element.13.stress, f32[256,256]{1,0:T(8,128)S(1)} %get-tuple-element.14.conc, ...), custom_call_target="tpu_custom_call" | custom-call | tf_op jit(solution)/shard_map/write/pallas_call | solution.py:703

commit v4 on v3

--- a/solution.py
+++ b/solution.py
@@ -295,7 +295,7 @@
             strip_columns(pl.multiple_of(own_at[half] + block * CHUNK, 8), CHUNK)
             return 0
 
-        lax.fori_loop(0, half_rows // CHUNK, own_columns, 0)
+        lax.fori_loop(0, half_rows // CHUNK, own_columns, 0, unroll=True)
     strip_columns(own_at[0] + half_rows, MARGIN)
     strip_columns(bases[1], MARGIN)
 
@@ -399,7 +399,7 @@
                        MARGIN + start, half * HALF)
             return 0
 
-        lax.fori_loop(0, half_rows // CHUNK, strip_own, 0)
+        lax.fori_loop(0, half_rows // CHUNK, strip_own, 0, unroll=True)
     strip_rows(half_rows, own_at[0] + half_rows, MARGIN, MARGIN, HALF)
     strip_rows(half_rows - MARGIN, bases[1], MARGIN, half_rows, 0)
     strip_columns(bases[0], MARGIN)
@@ -569,7 +569,7 @@
             )
             return 0
 
-        lax.fori_loop(0, half_rows // CHUNK, body, 0)
+        lax.fori_loop(0, half_rows // CHUNK, body, 0, unroll=True)
 
     early = (1 - me) if ens_count == 2 else jnp.int32(0)
     late = 1 - early

time: 45.3 us -> 45.2 us (level)
  no operation moved by 1% of the time
where the time goes in v4:
time: 45.2 us; the launch traced here: 45 us
  Pallas kernels  44.4 us (98%)
  between operations  0.64 us (1%)
    pallas_call x1, Pallas kernels, body(): pl.pallas_call(functools.partial(step_kernel, (gx_count, gy_count, ens_co...  43 us
    pallas_call x1, Pallas kernels, body(): pl.pallas_call(functools.partial(write_kernel, ens_count), name='write',...  1.34 us

profile of v4, /device:TPU:0, one launch (start us, length us, event | category | flops | bytes accessed | tf_op | source)
XLA Modules:
  0.0 45.0 jit_solution(8560607471460239038)
XLA Ops:
  0.6 43.0 %subcycles.1 = (f32[2,256,256]{2,1,0:T(8,128)S(1)}, f32[3,256,256]{2,1,0:T(8,128)S(1)}, f32[256,256]{1,0:T(8,128)S(1)}, f32[1,3,128,256]{3,2,1,0:T(8,128)S(1)}) custom-call(f32[2,256,256]{2,1,0:T(8,128)} %bitcast.11, f32[3,256,256]{2,1,0:T(8,128)} %bitcast.10, f32[256,256]{1,0:T(8,128)} %bitcast.14, f32[256,256]{1,0:T(8,128)} %bitcast.15, ...), custom_call_target="tpu_custom_call" | custom-call | tf_op jit(solution)/shard_map/subcycles/pallas_call | solution.py:669
  43.7 1.3 %write.1 = (f32[2,256,256]{2,1,0:T(8,128)}, f32[3,256,256]{2,1,0:T(8,128)}, f32[3,128,256]{2,1,0:T(8,128)}, f32[3,128,256]{2,1,0:T(8,128)}) custom-call(f32[2,256,256]{2,1,0:T(8,128)S(1)} %get-tuple-element.12.vel, f32[3,256,256]{2,1,0:T(8,128)S(1)} %get-tuple-element.13.stress, f32[256,256]{1,0:T(8,128)S(1)} %get-tuple-element.14.conc, ...), custom_call_target="tpu_custom_call" | custom-call | tf_op jit(solution)/shard_map/write/pallas_call | solution.py:703
